TPU v7x, 32 devices: a whole 2x2x4 slice. The times are simulated.
32 devices in a mesh: section: 2 (over y), dp: 4 (over x, core), mp: 4 (over z).
Axes of the slice: x: 2, y: 2, z: 4, core: 2. Of those that a mesh axis runs over, the one named last changes fastest.
Arguments:
- patches: bfloat16 [4096, 1280], P(('section', 'dp')), may hold values from -6 to 6
- patch_counts: int32 [16], P(('section', 'dp')), may hold values from 64 to 256, as said below
- dest_rows: int32 [1024], P(('section', 'dp')), may hold values from 0 to 4095, as said below
- qkv_weight: bfloat16 [1280, 3, 1280], P(None, None, 'mp'), may hold values from -1 to 1
- out_weight: bfloat16 [1280, 1280], P('mp'), may hold values from -0.15625 to 0.15625
- attn_gain: bfloat16 [1280], replicated, may hold values from 0.25 to 1.75
- merge_gain: bfloat16 [1280], replicated, may hold values from 0.25 to 1.75
- fc1_weight: bfloat16 [5120, 5120], P('mp', ('section', 'dp')), may hold values from -0.078125 to 0.078125
- fc1_bias: bfloat16 [5120], P(('section', 'dp')), may hold values from -3 to 3
- fc2_weight: bfloat16 [5120, 8192], P(('section', 'dp'), 'mp'), may hold values from -0.078125 to 0.078125
- fc2_bias: bfloat16 [8192], P('mp'), may hold values from -3 to 3
- text_embeds: bfloat16 [4096, 8192], P(('section', 'dp'), 'mp'), may hold values from -6 to 6
- section_hidden: bfloat16 [4096, 8192], P(('section', 'dp'), 'mp'), may hold values from -80 to 80
- llm_gain: bfloat16 [8192], P('mp'), may hold values from 0.25 to 1.75
Outputs:
- sequence_embeds: bfloat16 [4096, 8192], P(('section', 'dp'), 'mp')
- layer_inputs: bfloat16 [4096, 8192], P(('section', 'dp'), 'mp')
Inputs may be any that keep to these rules, and one draw needn't show every extreme that they name: `patch_counts`: multiples of 4; a tile's patches fill the first slots of its block. `dest_rows`: all rows differ. Each group's merged slots form runs of 16 consecutive slots (aligned); a run goes to one sequence slice (row // 512, numbered in section-major order), different runs of a group to different slices. Rows of slots that are not live are never written.
All inputs are finite; a program needn't handle non-finite values.
Results may differ from a plain program's by a relative error of at most 0.0055.
Values may be sent and summed in bfloat16 or wider, within the bound.
A program may use at most 128 MiB of HBM per device.

v0:
```python
import jax
import jax.numpy as jnp
from jax import lax
from jax.sharding import PartitionSpec as P

HEAD_DIM = 80
HID = 8192
vit_eps = 1e-06
llm_eps = 1e-06


def from_behind(value, axis, steps):
    count = lax.axis_size(axis)
    first, last = (max(0, -steps), min(count, count - steps))
    return lax.ppermute(value, axis, [(source, source + steps) for source in range(first, last)])


def layer_norm(values, gain):
    centred = values.astype(jnp.float32)
    centred = centred - jnp.mean(centred, axis=-1, keepdims=True)
    variance = jnp.mean(centred * centred, axis=-1, keepdims=True)
    return centred * lax.rsqrt(variance + vit_eps) * gain.astype(jnp.float32)


def per_device(
    patches,
    patch_counts,
    dest_rows,
    qkv_weight,
    out_weight,
    attn_gain,
    merge_gain,
    fc1_weight,
    fc1_bias,
    fc2_weight,
    fc2_bias,
    text_embeds,
    section_hidden,
    llm_gain,
):
    width = patches.shape[1]
    tile_total = patch_counts.shape[0]
    block_rows = patches.shape[0] // tile_total
    merged_rows = patches.shape[0] // 4
    local_cols = qkv_weight.shape[2]
    local_heads = local_cols // HEAD_DIM
    feature_cols = text_embeds.shape[1]
    seq_rows = text_embeds.shape[0]
    section_count = lax.axis_size("section")
    group_count = section_count * lax.axis_size("dp")
    run_cap = max(2, merged_rows // group_count)
    run_total = merged_rows // run_cap
    normed_in = layer_norm(patches, attn_gain).astype(jnp.bfloat16)
    projections = jnp.dot(
        normed_in, qkv_weight.reshape(width, 3 * local_cols), preferred_element_type=jnp.float32
    ).astype(jnp.bfloat16)
    projections = projections.reshape(tile_total, block_rows, 3, local_heads, HEAD_DIM)
    query_part = projections[:, :, 0]
    key_part = projections[:, :, 1]
    value_part = projections[:, :, 2]
    scores = jnp.einsum(
        "tqhd,tkhd->thqk", query_part, key_part, preferred_element_type=jnp.float32
    ) * HEAD_DIM ** (-0.5)
    key_live = (
        jnp.arange(block_rows, dtype=jnp.int32)[None, None, None, :]
        < patch_counts[:, None, None, None]
    )
    scores = jnp.where(key_live, scores, -1e30)
    weights = jax.nn.softmax(scores, axis=-1).astype(jnp.bfloat16)
    attended = jnp.einsum(
        "thqk,tkhd->tqhd", weights, value_part, preferred_element_type=jnp.float32
    ).astype(jnp.bfloat16)
    attended = attended.reshape(patches.shape[0], local_cols)
    partial_proj = jnp.dot(attended, out_weight, preferred_element_type=jnp.float32)
    position = lax.axis_index("mp")
    own_patch = lax.dynamic_slice_in_dim(
        patches.reshape(merged_rows, 4, width), position, 1, 1
    ).reshape(merged_rows, width)
    own_proj = lax.psum_scatter(
        partial_proj.reshape(merged_rows, 4, width), "mp", scatter_dimension=1, tiled=True
    ).reshape(merged_rows, width)
    block_out = (own_patch.astype(jnp.float32) + own_proj).astype(jnp.bfloat16)
    merge_part = layer_norm(block_out, merge_gain).astype(jnp.bfloat16)
    first_full, second_full, bias_full = (
        lax.all_gather(fc1_weight, "section", axis=1, tiled=True),
        lax.all_gather(fc2_weight, "section", axis=0, tiled=True),
        lax.all_gather(fc1_bias, "section", axis=0, tiled=True),
    )
    first_partial = jnp.dot(
        lax.all_gather(merge_part, "dp", axis=0, tiled=True),
        first_full,
        preferred_element_type=jnp.float32,
    )
    first_total = lax.psum(first_partial, "mp")
    hidden = jax.nn.gelu(first_total + bias_full.astype(jnp.float32), approximate=False).astype(
        jnp.bfloat16
    )
    embed_total = lax.psum_scatter(
        jnp.dot(hidden, second_full, preferred_element_type=jnp.float32).astype(jnp.bfloat16),
        "dp",
        scatter_dimension=0,
        tiled=True,
    ).astype(jnp.float32)
    image_embeds = (embed_total + fc2_bias.astype(jnp.float32)).astype(jnp.bfloat16)
    slot_in_tile = jnp.arange(merged_rows, dtype=jnp.int32) % (block_rows // 4)
    tile_counts = jnp.repeat(patch_counts, block_rows // 4, total_repeat_length=merged_rows)
    live = slot_in_tile * 4 < tile_counts
    receiver = dest_rows // seq_rows
    run_target = receiver.reshape(run_total, run_cap)[:, 0]
    place = jnp.where(live, dest_rows % seq_rows, seq_rows)
    send_rows = (
        jnp.zeros((group_count, run_cap, feature_cols), jnp.bfloat16)
        .at[run_target]
        .set(image_embeds.reshape(run_total, run_cap, feature_cols))
    )
    send_place = (
        jnp.full((group_count, run_cap), seq_rows, jnp.int32)
        .at[run_target]
        .set(place.reshape(run_total, run_cap))
    )
    got_rows, got_place = (
        lax.all_to_all(send_rows, ("section", "dp"), split_axis=0, concat_axis=0, tiled=True),
        lax.all_to_all(send_place, ("section", "dp"), split_axis=0, concat_axis=0, tiled=True),
    )
    sequence_embeds = text_embeds.at[got_place.reshape(-1)].set(
        got_rows.reshape(-1, feature_cols), mode="drop"
    )
    incoming = from_behind(section_hidden, "section", 1)
    entering = jnp.where(lax.axis_index("section") == 0, sequence_embeds, incoming).astype(
        jnp.float32
    )
    row_total = lax.psum(jnp.sum(entering * entering, axis=1), "mp")
    layer_inputs = (
        entering * lax.rsqrt(row_total / HID + llm_eps)[:, None] * llm_gain.astype(jnp.float32)
    ).astype(jnp.bfloat16)
    return (sequence_embeds, layer_inputs)


def solution(mesh):
    in_specs = (
        P(("section", "dp"), None),
        P(("section", "dp")),
        P(("section", "dp")),
        P(None, None, "mp"),
        P("mp", None),
        P(),
        P(),
        P("mp", ("section", "dp")),
        P(("section", "dp")),
        P(("section", "dp"), "mp"),
        P("mp"),
        P(("section", "dp"), "mp"),
        P(("section", "dp"), "mp"),
        P("mp"),
    )
    out_specs = (P(("section", "dp"), "mp"), P(("section", "dp"), "mp"))
    return jax.shard_map(
        per_device, mesh=mesh, in_specs=in_specs, out_specs=out_specs, check_vma=False
    )
```

profile of v0, /device:TPU:0, one launch (start us, length us, event | category | flops | bytes accessed | tf_op | source)
XLA Modules:
  0.0 317.5 jit_solution(10290408837068384715)
XLA Ops:
  8.1 3.3 %copy.70 = bf16[512,2048]{1,0:T(8,128)(2,1)} copy(bf16[512,2048]{1,0:T(8,128)(2,1)} %param.27) | data formatting | bytes 4194304
  11.4 0.2 convert_reduce_fusion
  11.7 0.5 fusion.6
  12.2 2.6 convolution_convert_fusion.1
  14.8 2.5 reshape.162
  17.3 1.6 fusion.107
  18.9 3.3 %fusion.109 = (f32[2,4,256]{2,1,0:T(4,128)S(1)}, f32[2,4,256,256]{2,3,1,0:T(8,128)}) fusion(pred[2,256]{1,0:T(4,128)(4,1)S(1)} %iota_compare_fusion, bf16[2,256,1,4,80]{1,0,4,3,2:T(2,128)(2,1)} %get-tuple-element.18, bf16[2,256,1,4,80]{1,0,4,3,2:T(2,128)(2,1)} %get-tuple-element.17), kind=kOutput, calls=%fused_computation.154 | convolution fusion | flops 85983488 | bytes 2761216 | tf_op jit(solution)/shard_map/sub | solution.py:69
  22.2 1.9 fusion.56
  24.1 0.3 copy.33
  24.4 0.5 dot_general.23
  24.9 3.5 %fusion.60 = f32[128,4,1280]{2,0,1:T(8,128)} fusion(bf16[320,1280]{1,0:T(8,128)(2,1)} %param.20, bf16[128,4,320]{2,1,0:T(4,128)(2,1)S(1)} %dot_general.23), kind=kOutput, calls=%fused_computation.82 | convolution fusion | flops 419430400 | bytes 3768320 | tf_op jit(solution)/shard_map/dot_general | solution.py:74
  28.5 0.5 all-gather.7.cloned.1.call-update
  29.1 3.5 %reshape.160 = bf16[128,4,1280]{2,1,0:T(4,128)(2,1)} reshape(bf16[512,1280]{1,0:T(8,128)(2,1)} %param.16) | data formatting | bytes 2621440 | tf_op jit(solution)/shard_map/reshape | solution.py:77
  32.6 2.0 constant_dynamic-slice_fusion
  34.6 49.0 %reduce-scatter.3.cloned.1.call-done = f32[128,1,1280]{2,0,1:T(8,128)} async-done(((f32[128,4,1280]{2,0,1:T(8,128)}), f32[128,1,1280]{2,0,1:T(8,128)}) %reduce-scatter.3.cloned.1.call-update) | async-done | bytes 655376 | tf_op jit(solution)/shard_map/reduce_scatter | solution.py:79
  83.6 1.2 convert_reduce_fusion.1
  84.8 0.2 fusion.65
  85.1 1.0 fusion.67
  86.1 0.5 all-gather.9.cloned.1.call-update
  86.7 17.1 %all-gather.5.cloned.1.call-done = bf16[512,1280]{1,0:T(8,128)(2,1)} async-done(((bf16[128,1280]{1,0:T(8,128)(2,1)}), bf16[512,1280]{1,0:T(8,128)(2,1)}) %all-gather.5.cloned.1.call-update) | async-done | bytes 1310736 | tf_op jit(solution)/shard_map/all_gather | solution.py:90
  103.8 5.8 %fusion.110 = f32[512,1280]{1,0:T(8,128)} fusion(bf16[512,1280]{1,0:T(8,128)(2,1)} %all-gather.5.cloned.1.call-done, bf16[1280,1280]{1,0:T(8,128)(2,1)} %all-gather.7.cloned.1.call-done), kind=kOutput, calls=%fused_computation.155 | convolution fusion | flops 1677721600 | bytes 7208960 | tf_op jit(solution)/shard_map/dot_general | solution.py:89
  109.6 0.6 copy-done.7
  110.2 4.5 %all-gather = bf16[2,1,640]{2,1,0:T(2,128)(2,1)S(1)} all-gather(bf16[1,1,640]{2,1,0:T(2,128)(2,1)S(1)} %reshape.198), channel_id=1, replica_groups=mesh['section'=2,'dp'=4,'mp'=4] {'section'}, dimensions={0}, use_global_device_ids=true | all-gather | bytes 3840 | tf_op jit(solution)/shard_map/all_gather | solution.py:87
  114.8 58.8 %all-gather.9.cloned.1.call-done = bf16[1280,2048]{1,0:T(8,128)(2,1)} async-done(((bf16[640,2048]{1,0:T(8,128)(2,1)}), bf16[1280,2048]{1,0:T(8,128)(2,1)}) %all-gather.9.cloned.1.call-update) | async-done | bytes 5242896 | tf_op jit(solution)/shard_map/all_gather | solution.py:86
  173.6 40.2 %all-reduce.2.cloned.1.call-done = f32[512,1280]{1,0:T(8,128)} async-done(((f32[512,1280]{1,0:T(8,128)}), f32[512,1280]{1,0:T(8,128)}) %all-reduce.2.cloned.1.call-update) | async-done | bytes 2621456 | tf_op jit(solution)/shard_map/psum | solution.py:94
  213.8 12.1 %convolution_convert_fusion = bf16[512,2048]{1,0:T(8,128)(2,1)} fusion(bf16[1280,2048]{1,0:T(8,128)(2,1)} %all-gather.9.cloned.1.call-done, f32[512,1280]{1,0:T(8,128)} %all-reduce.2.cloned.1.call-done, f32[1280]{0:T(1024)S(1)} %reshape.200), kind=kOutput, calls=%fused_computation.14 | convolution fusion | flops 2728656896 | bytes 9966592 | tf_op jit(solution)/shard_map/dot_general | solution.py:99
  225.9 4.7 %collective-permute-start = (bf16[512,2048]{1,0:T(8,128)(2,1)}, bf16[512,2048]{1,0:T(8,128)(2,1)}, u32[]{:S(2)}, u32[]{:S(2)}) collective-permute-start(bf16[512,2048]{1,0:T(8,128)(2,1)} %param.28), channel_id=1, source_target_pairs={{0,16},{1,17},{2,18},{3,19},{4,20},{5,21},{6,22},{7,23},{8,24},{9,... | collective-permute-start | bytes 6291464 | tf_op jit(solution)/shard_map/ppermute | solution.py:15
  230.7 0.6 fusion.108
  231.3 1.3 compare_select_fusion.2
  232.6 0.1 reshape.157
  232.6 0.1 reshape.178
  232.7 0.1 fusion.70
  232.8 1.2 scatter_custom_fusion
  234.0 3.3 %all-to-all-start = ((s32[8,1,16]{2,1,0:T(1,128)}), s32[8,1,16]{2,1,0:T(1,128)S(1)}, u32[]{:S(2)}, u32[]{:S(2)}) async-start(s32[8,1,16]{2,1,0:T(1,128)} %bitcast.3), calls=%async_computation | async-start | bytes 8192 | tf_op jit(solution)/shard_map/all_to_all | solution.py:123
  237.3 19.0 %reduce-scatter.5.cloned.1.call-done = bf16[128,2048]{1,0:T(8,128)(2,1)} async-done(((bf16[512,2048]{1,0:T(8,128)(2,1)}), bf16[128,2048]{1,0:T(8,128)(2,1)}) %reduce-scatter.5.cloned.1.call-update) | async-done | bytes 524304 | tf_op jit(solution)/shard_map/reduce_scatter | solution.py:98
  256.3 1.1 add_convert_fusion
  257.4 0.8 broadcast_in_dim.20
  258.3 2.4 scatter_fusion
  260.7 13.7 %all-to-all-done = s32[8,1,16]{2,1,0:T(1,128)S(1)} async-done(((s32[8,1,16]{2,1,0:T(1,128)}), s32[8,1,16]{2,1,0:T(1,128)S(1)}, u32[]{:S(2)}, u32[]{:S(2)}) %all-to-all-start) | async-done | bytes 544 | tf_op jit(solution)/shard_map/all_to_all | solution.py:123
  274.4 4.7 %all-to-all-start.1 = ((bf16[8,16,2048]{2,1,0:T(8,128)(2,1)}), bf16[8,16,2048]{2,1,0:T(8,128)(2,1)S(1)}, u32[]{:S(2)}, u32[]{:S(2)}) async-start(bf16[8,16,2048]{2,1,0:T(8,128)(2,1)} %scatter_fusion), calls=%async_computation.3 | async-start | bytes 1048576 | tf_op jit(solution)/shard_map/all_to_all | solution.py:122
  279.1 0.5 broadcast.190
  279.6 0.6 reduce.10
  280.2 0.1 reshape.159
  280.3 8.5 %all-to-all-done.1 = bf16[8,16,2048]{2,1,0:T(8,128)(2,1)S(1)} async-done(((bf16[8,16,2048]{2,1,0:T(8,128)(2,1)}), bf16[8,16,2048]{2,1,0:T(8,128)(2,1)S(1)}, u32[]{:S(2)}, u32[]{:S(2)}) %all-to-all-start.1) | async-done | bytes 524320 | tf_op jit(solution)/shard_map/all_to_all | solution.py:122
  288.8 4.6 %scatter_fusion.1 = bf16[512,2048]{1,0:T(8,128)(2,1)} fusion(bf16[512,2048]{1,0:T(8,128)(2,1)} %copy.70, s32[128]{0:T(128)S(1)} %fusion.74, bf16[128,2048]{1,0:T(8,128)(2,1)S(1)} %bitcast.61), kind=kCustom, calls=%fused_computation.2 | custom fusion | bytes 1573376 | tf_op jit(solution)/shard_map/scatter | solution.py:125
  293.4 2.3 fusion.1
  295.7 10.0 %psum.15 = f32[512]{0:T(512)S(1)} all-reduce(f32[512]{0:T(512)S(1)} %fusion.1), channel_id=1, replica_groups=mesh['section'=2,'dp'=4,'mp'=4] {'mp'}, use_global_device_ids=true, to_apply=%region_13.14 | all-reduce | flops 512 | bytes 4096 | tf_op jit(solution)/shard_map/psum | solution.py:132
  305.8 4.1 %fusion.3 = bf16[512,2048]{1,0:T(8,128)(2,1)} fusion(f32[2048]{0:T(1024)S(1)} %convert_element_type.88, f32[512]{0:T(512)S(1)} %add_rsqrt_fusion, bf16[512,2048]{1,0:T(8,128)(2,1)} %scatter_fusion.1, bf16[512,2048]{1,0:T(8,128)(2,1)} %collective-permute-done, pred[]{:T(512)S(6)} %eq.6), kind=kLoop, calls=%fused_computation.8 | loop fusion | flops 5242880 | bytes 6301697 | tf_op jit(solution)/shard_map/convert_element_type | solution.py:135
  (47 shorter events, 0.6 us)
Async XLA Ops:
  8.0 4.2 %copy-start = (bf16[1280,3,320]{0,2,1:T(8,128)(2,1)S(1)}, bf16[1280,3,320]{0,2,1:T(8,128)(2,1)}, u32[]{:S(2)}) copy-start(bf16[1280,3,320]{0,2,1:T(8,128)(2,1)} %param.19) | copy-start | bytes 7372804
  8.0 4.1 %copy-start.3 = (bf16[1280]{0:T(1024)(128)(2,1)S(1)}, bf16[1280]{0:T(1024)(128)(2,1)}, u32[]{:S(2)}) copy-start(bf16[1280]{0:T(1024)(128)(2,1)} %param.21) | copy-start | bytes 7684
  8.0 75.6 %reduce-scatter.3.cloned.1.call-start = ((), (), s32[]{:S(2)}) async-start(), calls=%async_computation.4 | async-start | bytes 3276800 | tf_op jit(solution)/shard_map/reduce_scatter | solution.py:79
  8.1 3.3 %copy-start.1 = (bf16[512,1280]{1,0:T(8,128)(2,1)S(1)}, bf16[512,1280]{1,0:T(8,128)(2,1)}, u32[]{:S(2)}) copy-start(bf16[512,1280]{1,0:T(8,128)(2,1)} %param.16) | copy-start | bytes 3932164
  14.8 4.1 %copy-start.8 = (s32[2]{0:T(128)S(1)}, s32[2]{0:T(128)}, u32[]{:S(2)}) copy-start(s32[2]{0:T(128)} %param.17) | copy-start | bytes 28
  18.9 3.4 %copy-start.2 = (bf16[2,256,1,4,80]{1,0,4,3,2:T(2,128)(2,1)S(1)}, bf16[2,256,1,4,80]{1,0,4,3,2:T(2,128)(2,1)}, u32[]{:S(2)}) copy-start(bf16[2,256,1,4,80]{1,0,4,3,2:T(2,128)(2,1)} %get-tuple-element.16) | copy-start | bytes 983044
  28.5 4.1 %copy-start.4 = (bf16[1280]{0:T(1024)(128)(2,1)S(1)}, bf16[1280]{0:T(1024)(128)(2,1)}, u32[]{:S(2)}) copy-start(bf16[1280]{0:T(1024)(128)(2,1)} %param.22) | copy-start | bytes 7684
  28.5 58.3 %all-gather.7.cloned.1.call-start = ((), (), s32[]{:S(2)}) async-start(), calls=%async_computation.6 | async-start | bytes 4915200 | tf_op jit(solution)/shard_map/all_gather | solution.py:85
  29.1 74.7 %all-gather.5.cloned.1.call-start = ((), (), s32[]{:S(2)}) async-start(), calls=%async_computation.5 | async-start | bytes 1638400 | tf_op jit(solution)/shard_map/all_gather | solution.py:90
  86.1 87.6 %all-gather.9.cloned.1.call-start = ((), (), s32[]{:S(2)}) async-start(), calls=%async_computation.8 | async-start | bytes 7864320 | tf_op jit(solution)/shard_map/all_gather | solution.py:86
  86.6 127.2 %all-reduce.2.cloned.1.call-start = ((), (), s32[]{:S(2)}) async-start(), calls=%async_computation.7 | async-start | bytes 5242880 | tf_op jit(solution)/shard_map/psum | solution.py:94
  109.5 0.7 copy-start.7
  109.6 146.7 %reduce-scatter.5.cloned.1.call-start = ((), (), s32[]{:S(2)}) async-start(), calls=%async_computation.9 | async-start | bytes 2621440 | tf_op jit(solution)/shard_map/reduce_scatter | solution.py:98
  114.8 116.5 %copy-start.9 = (s32[128]{0:T(128)S(1)}, s32[128]{0:T(128)}, u32[]{:S(2)}) copy-start(s32[128]{0:T(128)} %param.18) | copy-start | bytes 1540
  114.8 116.5 %copy-start.10 = (pred[128]{0:T(512)(128)(4,1)S(1)}, pred[128]{0:T(512)(128)(4,1)}, u32[]{:S(2)}) copy-start(pred[128]{0:T(512)(128)(4,1)} %constant.224) | copy-start | bytes 388
  114.8 122.4 %copy-start.5 = (bf16[2048]{0:T(1024)(128)(2,1)S(1)}, bf16[2048]{0:T(1024)(128)(2,1)}, u32[]{:S(2)}) copy-start(bf16[2048]{0:T(1024)(128)(2,1)} %param.26) | copy-start | bytes 12292
  225.9 53.1 %copy-start.6 = (bf16[2048]{0:T(1024)(128)(2,1)S(1)}, bf16[2048]{0:T(1024)(128)(2,1)}, u32[]{:S(2)}) copy-start(bf16[2048]{0:T(1024)(128)(2,1)} %param.29) | copy-start | bytes 12292
  225.9 67.4 %collective-permute-start = (bf16[512,2048]{1,0:T(8,128)(2,1)}, bf16[512,2048]{1,0:T(8,128)(2,1)}, u32[]{:S(2)}, u32[]{:S(2)}) collective-permute-start(bf16[512,2048]{1,0:T(8,128)(2,1)} %param.28), channel_id=1, source_target_pairs={{0,16},{1,17},{2,18},{3,19},{4,20},{5,21},{6,22},{7,23},{8,24},{9,... | collective-permute-start | bytes 6291464 | tf_op jit(solution)/shard_map/ppermute | solution.py:15
  234.0 40.4 %all-to-all-start = ((s32[8,1,16]{2,1,0:T(1,128)}), s32[8,1,16]{2,1,0:T(1,128)S(1)}, u32[]{:S(2)}, u32[]{:S(2)}) async-start(s32[8,1,16]{2,1,0:T(1,128)} %bitcast.3), calls=%async_computation | async-start | bytes 8192 | tf_op jit(solution)/shard_map/all_to_all | solution.py:123
  274.4 14.4 %all-to-all-start.1 = ((bf16[8,16,2048]{2,1,0:T(8,128)(2,1)}), bf16[8,16,2048]{2,1,0:T(8,128)(2,1)S(1)}, u32[]{:S(2)}, u32[]{:S(2)}) async-start(bf16[8,16,2048]{2,1,0:T(8,128)(2,1)} %scatter_fusion), calls=%async_computation.3 | async-start | bytes 1048576 | tf_op jit(solution)/shard_map/all_to_all | solution.py:122
Sparse Core Ops, SparseCore 0:
  28.6 54.9 reduce-scatter.2
  109.7 104.0 all-reduce.1
Sparse Core Ops, SparseCore 1:
  30.5 48.9 all-gather.6
  86.2 17.6 all-gather.4
  105.2 68.4 all-gather.8
  226.0 30.2 reduce-scatter.4
where the time goes:
time: 318 us; the launch traced here: 317 us
  waiting for transfers between devices  207 us (65%)
  matrix products  29.1 us (9%)
  local copies, waits for them, and re-layouts  24.8 us (8%)
  between operations  15.9 us (5%)
  blocking collectives  14.6 us (5%)
  starting transfers between devices  12.9 us (4%)
  other arithmetic  12.9 us (4%)
    all_gather x1, waiting for transfers between devices, per_device(): lax.all_gather(fc2_weight, 'section', axis=0, tiled=True)  58.8 us
    reduce_scatter x1, waiting for transfers between devices, per_device(): lax.psum_scatter(partial_proj.reshape(merged_rows, 4, width), 'mp', scatt...  49 us
    psum x1, waiting for transfers between devices, per_device(): first_total = lax.psum(first_partial, 'mp')  40.2 us
    reduce_scatter x1, waiting for transfers between devices, per_device(): lax.psum_scatter(jnp.dot(hidden, second_full, preferred_element_type=jnp....  19 us
    all_gather x1, waiting for transfers between devices, per_device(): lax.all_gather(merge_part, 'dp', axis=0, tiled=True)  17.1 us
    all_to_all x1, waiting for transfers between devices, per_device(): lax.all_to_all(send_place, ('section', 'dp'), split_axis=0, concat_axis=0...  13.7 us
    dot_general x1, matrix products, per_device(): jnp.dot(hidden, second_full, preferred_element_type=jnp.float32)  12.1 us
    psum x1, blocking collectives, per_device(): row_total = lax.psum(jnp.sum(entering * entering, axis=1), 'mp')  10 us
  transfers between devices with their start and end apart: 9, of which 7 were waited for; matrix products, arithmetic and copies ran while one was open for 9% of the time, Pallas kernels for 0%

commit v1 on v0

--- a/solution.py
+++ b/solution.py
@@ -91,7 +91,11 @@
         first_full,
         preferred_element_type=jnp.float32,
     )
-    first_total = lax.psum(first_partial, "mp")
+    first_total = first_partial
+    for hop in (1, 2):
+        first_total = first_total + lax.ppermute(
+            first_total, "mp", [(dev, dev ^ hop) for dev in range(4)]
+        )
     hidden = jax.nn.gelu(first_total + bias_full.astype(jnp.float32), approximate=False).astype(
         jnp.bfloat16
     )

time: 318 us -> 395 us (1.24)
  waiting for transfers between devices: 207 us -> 274 us
  other arithmetic: 12.9 us -> 17.3 us
    ppermute x0 -> x2, waiting for transfers between devices: none -> 166 us  [per_device(): lax.ppermute(first_total, 'mp', [(dev, dev ^ hop) for dev in range(4)])]
    all_gather x1, waiting for transfers between devices: 58.8 us -> 0.03 us  [per_device(): lax.all_gather(fc2_weight, 'section', axis=0, tiled=True)]
    psum x1 -> x0, waiting for transfers between devices: 40.2 us -> none  [per_device(): first_total = lax.psum(first_partial, 'mp')]
    add x0 -> x1, other arithmetic: none -> 4.34 us  [per_device(): first_total + lax.ppermute(first_total, 'mp', [(dev, dev ^ hop) for dev i...]
  transfers between devices with their start and end apart: 9 -> 10, of which waited for: 7 -> 7; matrix products, arithmetic and copies ran while one was open for 9% -> 7% of each run, Pallas kernels for 0% -> 0%
where the time goes in v1:
time: 395 us; the launch traced here: 394 us
  waiting for transfers between devices  274 us (69%)
  matrix products  29.6 us (7%)
  local copies, waits for them, and re-layouts  24.2 us (6%)
  other arithmetic  17.3 us (4%)
  blocking collectives  17.1 us (4%)
  starting transfers between devices  15.9 us (4%)
  between operations  15.9 us (4%)
    ppermute x2, waiting for transfers between devices, per_device(): lax.ppermute(first_total, 'mp', [(dev, dev ^ hop) for dev in range(4)])  166 us
    reduce_scatter x1, waiting for transfers between devices, per_device(): lax.psum_scatter(partial_proj.reshape(merged_rows, 4, width), 'mp', scatt...  49 us
    reduce_scatter x1, waiting for transfers between devices, per_device(): lax.psum_scatter(jnp.dot(hidden, second_full, preferred_element_type=jnp....  19.8 us
    all_gather x1, waiting for transfers between devices, per_device(): lax.all_gather(merge_part, 'dp', axis=0, tiled=True)  17.6 us
    dot_general x1, matrix products, per_device(): jnp.dot(hidden, second_full, preferred_element_type=jnp.float32)  12.6 us
    psum x1, blocking collectives, per_device(): row_total = lax.psum(jnp.sum(entering * entering, axis=1), 'mp')  12.6 us
    all_to_all x1, waiting for transfers between devices, per_device(): lax.all_to_all(send_place, ('section', 'dp'), split_axis=0, concat_axis=0...  12.3 us
    all_to_all x1, waiting for transfers between devices, per_device(): lax.all_to_all(send_rows, ('section', 'dp'), split_axis=0, concat_axis=0,...  8.45 us
  transfers between devices with their start and end apart: 10, of which 7 were waited for; matrix products, arithmetic and copies ran while one was open for 7% of the time, Pallas kernels for 0%

profile of v1, /device:TPU:0, one launch (start us, length us, event | category | flops | bytes accessed | tf_op | source)
XLA Modules:
  0.0 394.0 jit_solution(4654952679062901406)
XLA Ops:
  8.1 3.3 copy.69
  11.4 0.2 convert_reduce_fusion
  11.7 0.5 fusion.6
  12.2 2.6 convolution_convert_fusion.1
  14.8 2.5 reshape.162
  17.3 1.6 fusion.107
  18.9 3.3 fusion.109
  22.2 1.9 fusion.56
  24.1 0.3 copy.33
  24.4 0.5 dot_general.23
  24.9 3.5 fusion.60
  28.6 0.5 all-gather.7.cloned.1.call-update
  29.1 3.5 reshape.160
  32.6 2.0 constant_dynamic-slice_fusion
  34.6 49.0 %reduce-scatter.3.cloned.1.call-done = f32[128,1,1280]{2,0,1:T(8,128)} async-done(((f32[128,4,1280]{2,0,1:T(8,128)}), f32[128,1,1280]{2,0,1:T(8,128)}) %reduce-scatter.3.cloned.1.call-update) | async-done | bytes 655376 | tf_op jit(solution)/shard_map/reduce_scatter | solution.py:79
  83.6 1.2 convert_reduce_fusion.1
  84.9 0.2 fusion.65
  85.1 1.0 fusion.67
  86.2 17.6 %all-gather.5.cloned.1.call-done = bf16[512,1280]{1,0:T(8,128)(2,1)} async-done(((bf16[128,1280]{1,0:T(8,128)(2,1)}), bf16[512,1280]{1,0:T(8,128)(2,1)}) %all-gather.5.cloned.1.call-update) | async-done | bytes 1310736 | tf_op jit(solution)/shard_map/all_gather | solution.py:90
  103.8 5.7 %fusion.110 = f32[512,1280]{1,0:T(8,128)} fusion(bf16[512,1280]{1,0:T(8,128)(2,1)} %all-gather.5.cloned.1.call-done, bf16[1280,1280]{1,0:T(8,128)(2,1)} %all-gather.7.cloned.1.call-done), kind=kOutput, calls=%fused_computation.156 | convolution fusion | flops 1677721600 | bytes 7208960 | tf_op jit(solution)/shard_map/dot_general | solution.py:89
  109.5 1.5 collective-permute-start
  111.1 57.7 %collective-permute-done = f32[512,1280]{1,0:T(8,128)} collective-permute-done((f32[512,1280]{1,0:T(8,128)}, f32[512,1280]{1,0:T(8,128)}, u32[]{:S(2)}, u32[]{:S(2)}) %collective-permute-start) | collective-permute-done | bytes 2621472 | tf_op jit(solution)/shard_map/ppermute | solution.py:96
  168.8 4.3 %add.114 = f32[512,1280]{1,0:T(8,128)} add(f32[512,1280]{1,0:T(8,128)} %fusion.110, f32[512,1280]{1,0:T(8,128)} %collective-permute-done) | non-fusion elementwise | flops 655360 | bytes 7864320 | tf_op jit(solution)/shard_map/add | solution.py:96
  173.2 2.4 collective-permute-start.1
  175.6 4.5 %all-gather = bf16[2,1,640]{2,1,0:T(2,128)(2,1)S(1)} all-gather(bf16[1,1,640]{2,1,0:T(2,128)(2,1)S(1)} %reshape.198), channel_id=1, replica_groups=mesh['section'=2,'dp'=4,'mp'=4] {'section'}, dimensions={0}, use_global_device_ids=true | all-gather | bytes 3840 | tf_op jit(solution)/shard_map/all_gather | solution.py:87
  180.2 108.5 %collective-permute-done.1 = f32[512,1280]{1,0:T(8,128)} collective-permute-done((f32[512,1280]{1,0:T(8,128)}, f32[512,1280]{1,0:T(8,128)}, u32[]{:S(2)}, u32[]{:S(2)}) %collective-permute-start.1) | collective-permute-done | bytes 2621472 | tf_op jit(solution)/shard_map/ppermute | solution.py:96
  288.7 12.6 %convolution_convert_fusion = bf16[512,2048]{1,0:T(8,128)(2,1)} fusion(bf16[1280,2048]{1,0:T(8,128)(2,1)} %all-gather.9.cloned.1.call-done, f32[512,1280]{1,0:T(8,128)} %add.114, f32[512,1280]{1,0:T(8,128)} %collective-permute-done.1, f32[1280]{0:T(1024)S(1)} %reshape.200), kind=kOutput, calls=%fused_computation.14 | convolution fusion | flops 2729312256 | bytes 12588032 | tf_op jit(solution)/shard_map/dot_general | solution.py:103
  301.3 4.7 %collective-permute-start.2 = (bf16[512,2048]{1,0:T(8,128)(2,1)}, bf16[512,2048]{1,0:T(8,128)(2,1)}, u32[]{:S(2)}, u32[]{:S(2)}) collective-permute-start(bf16[512,2048]{1,0:T(8,128)(2,1)} %param.28), channel_id=1, source_target_pairs={{0,16},{1,17},{2,18},{3,19},{4,20},{5,21},{6,22},{7,23},{8,24},{9,... | collective-permute-start | bytes 6291464 | tf_op jit(solution)/shard_map/ppermute | solution.py:15
  306.1 0.6 fusion.108
  306.7 1.3 compare_select_fusion.2
  308.0 0.1 reshape.157
  308.1 0.1 fusion.70
  308.2 1.2 scatter_custom_fusion
  309.4 3.3 all-to-all-start
  312.7 19.8 %reduce-scatter.5.cloned.1.call-done = bf16[128,2048]{1,0:T(8,128)(2,1)} async-done(((bf16[512,2048]{1,0:T(8,128)(2,1)}), bf16[128,2048]{1,0:T(8,128)(2,1)}) %reduce-scatter.5.cloned.1.call-update) | async-done | bytes 524304 | tf_op jit(solution)/shard_map/reduce_scatter | solution.py:102
  332.5 1.1 add_convert_fusion
  333.7 0.8 broadcast_in_dim.20
  334.5 2.4 scatter_fusion
  336.9 12.3 %all-to-all-done = s32[8,1,16]{2,1,0:T(1,128)S(1)} async-done(((s32[8,1,16]{2,1,0:T(1,128)}), s32[8,1,16]{2,1,0:T(1,128)S(1)}, u32[]{:S(2)}, u32[]{:S(2)}) %all-to-all-start) | async-done | bytes 544 | tf_op jit(solution)/shard_map/all_to_all | solution.py:127
  349.2 3.8 all-to-all-start.1
  353.0 0.5 broadcast.190
  353.5 0.6 reduce.10
  354.1 0.1 reshape.159
  354.2 8.5 %all-to-all-done.1 = bf16[8,16,2048]{2,1,0:T(8,128)(2,1)S(1)} async-done(((bf16[8,16,2048]{2,1,0:T(8,128)(2,1)}), bf16[8,16,2048]{2,1,0:T(8,128)(2,1)S(1)}, u32[]{:S(2)}, u32[]{:S(2)}) %all-to-all-start.1) | async-done | bytes 524320 | tf_op jit(solution)/shard_map/all_to_all | solution.py:126
  362.7 4.6 %scatter_fusion.1 = bf16[512,2048]{1,0:T(8,128)(2,1)} fusion(bf16[512,2048]{1,0:T(8,128)(2,1)} %copy.69, s32[128]{0:T(128)S(1)} %fusion.74, bf16[128,2048]{1,0:T(8,128)(2,1)S(1)} %bitcast.61), kind=kCustom, calls=%fused_computation.2 | custom fusion | bytes 1573376 | tf_op jit(solution)/shard_map/scatter | solution.py:129
  367.3 2.3 fusion.1
  369.6 12.6 %psum.7 = f32[512]{0:T(512)S(1)} all-reduce(f32[512]{0:T(512)S(1)} %fusion.1), channel_id=1, replica_groups=mesh['section'=2,'dp'=4,'mp'=4] {'mp'}, use_global_device_ids=true, to_apply=%region_12.13 | all-reduce | flops 512 | bytes 4096 | tf_op jit(solution)/shard_map/psum | solution.py:136
  382.2 4.1 %fusion.3 = bf16[512,2048]{1,0:T(8,128)(2,1)} fusion(f32[2048]{0:T(1024)S(1)} %convert_element_type.88, f32[512]{0:T(512)S(1)} %add_rsqrt_fusion, bf16[512,2048]{1,0:T(8,128)(2,1)} %scatter_fusion.1, bf16[512,2048]{1,0:T(8,128)(2,1)} %collective-permute-done.2, pred[]{:T(512)S(6)} %eq.6), kind=kLoop, calls=%fused_computation.8 | loop fusion | flops 5242880 | bytes 6301697 | tf_op jit(solution)/shard_map/convert_element_type | solution.py:139
  (49 shorter events, 0.6 us)
Async XLA Ops:
  8.0 4.2 %copy-start = (bf16[1280,3,320]{0,2,1:T(8,128)(2,1)S(1)}, bf16[1280,3,320]{0,2,1:T(8,128)(2,1)}, u32[]{:S(2)}) copy-start(bf16[1280,3,320]{0,2,1:T(8,128)(2,1)} %param.19) | copy-start | bytes 7372804
  8.0 4.1 %copy-start.3 = (bf16[1280]{0:T(1024)(128)(2,1)S(1)}, bf16[1280]{0:T(1024)(128)(2,1)}, u32[]{:S(2)}) copy-start(bf16[1280]{0:T(1024)(128)(2,1)} %param.21) | copy-start | bytes 7684
  8.0 75.6 %reduce-scatter.3.cloned.1.call-start = ((), (), s32[]{:S(2)}) async-start(), calls=%async_computation.4 | async-start | bytes 3276800 | tf_op jit(solution)/shard_map/reduce_scatter | solution.py:79
  8.1 3.3 copy-start.1
  14.8 4.1 %copy-start.8 = (s32[2]{0:T(128)S(1)}, s32[2]{0:T(128)}, u32[]{:S(2)}) copy-start(s32[2]{0:T(128)} %param.17) | copy-start | bytes 28
  18.9 3.4 copy-start.2
  28.5 4.1 %copy-start.4 = (bf16[1280]{0:T(1024)(128)(2,1)S(1)}, bf16[1280]{0:T(1024)(128)(2,1)}, u32[]{:S(2)}) copy-start(bf16[1280]{0:T(1024)(128)(2,1)} %param.22) | copy-start | bytes 7684
  28.5 57.7 %all-gather.7.cloned.1.call-start = ((), (), s32[]{:S(2)}) async-start(), calls=%async_computation.6 | async-start | bytes 4915200 | tf_op jit(solution)/shard_map/all_gather | solution.py:85
  29.1 74.7 %all-gather.5.cloned.1.call-start = ((), (), s32[]{:S(2)}) async-start(), calls=%async_computation.5 | async-start | bytes 1638400 | tf_op jit(solution)/shard_map/all_gather | solution.py:90
  86.1 94.1 %all-gather.9.cloned.1.call-start = ((), (), s32[]{:S(2)}) async-start(), calls=%async_computation.7 | async-start | bytes 7864320 | tf_op jit(solution)/shard_map/all_gather | solution.py:86
  109.5 59.3 %collective-permute-start = (f32[512,1280]{1,0:T(8,128)}, f32[512,1280]{1,0:T(8,128)}, u32[]{:S(2)}, u32[]{:S(2)}) collective-permute-start(f32[512,1280]{1,0:T(8,128)} %fusion.110), channel_id=1, source_target_pairs={{0,1},{1,0},{2,3},{3,2},{4,5},{5,4},{6,7},{7,6},{8,9},{9,8},{10,11... | collective-permute-start | bytes 7864328 | tf_op jit(solution)/shard_map/ppermute | solution.py:96
  111.0 64.6 %copy-start.7 = (bf16[640]{0:T(1024)(128)(2,1)S(1)}, bf16[640]{0:T(1024)(128)(2,1)}, u32[]{:S(2)}) copy-start(bf16[640]{0:T(1024)(128)(2,1)} %param.24) | copy-start | bytes 3844
  111.0 221.5 %reduce-scatter.5.cloned.1.call-start = ((), (), s32[]{:S(2)}) async-start(), calls=%async_computation.8 | async-start | bytes 2621440 | tf_op jit(solution)/shard_map/reduce_scatter | solution.py:102
  173.2 115.5 %collective-permute-start.1 = (f32[512,1280]{1,0:T(8,128)}, f32[512,1280]{1,0:T(8,128)}, u32[]{:S(2)}, u32[]{:S(2)}) collective-permute-start(f32[512,1280]{1,0:T(8,128)} %add.114), channel_id=1, source_target_pairs={{0,2},{1,3},{2,0},{3,1},{4,6},{5,7},{6,4},{7,5},{8,10},{9,11},{10,... | collective-permute-start | bytes 7864328 | tf_op jit(solution)/shard_map/ppermute | solution.py:96
  180.2 126.5 %copy-start.9 = (s32[128]{0:T(128)S(1)}, s32[128]{0:T(128)}, u32[]{:S(2)}) copy-start(s32[128]{0:T(128)} %param.18) | copy-start | bytes 1540
  180.2 126.5 %copy-start.10 = (pred[128]{0:T(512)(128)(4,1)S(1)}, pred[128]{0:T(512)(128)(4,1)}, u32[]{:S(2)}) copy-start(pred[128]{0:T(512)(128)(4,1)} %constant.224) | copy-start | bytes 388
  180.2 132.5 %copy-start.5 = (bf16[2048]{0:T(1024)(128)(2,1)S(1)}, bf16[2048]{0:T(1024)(128)(2,1)}, u32[]{:S(2)}) copy-start(bf16[2048]{0:T(1024)(128)(2,1)} %param.26) | copy-start | bytes 12292
  301.3 51.6 %copy-start.6 = (bf16[2048]{0:T(1024)(128)(2,1)S(1)}, bf16[2048]{0:T(1024)(128)(2,1)}, u32[]{:S(2)}) copy-start(bf16[2048]{0:T(1024)(128)(2,1)} %param.29) | copy-start | bytes 12292
  301.3 65.9 %collective-permute-start.2 = (bf16[512,2048]{1,0:T(8,128)(2,1)}, bf16[512,2048]{1,0:T(8,128)(2,1)}, u32[]{:S(2)}, u32[]{:S(2)}) collective-permute-start(bf16[512,2048]{1,0:T(8,128)(2,1)} %param.28), channel_id=1, source_target_pairs={{0,16},{1,17},{2,18},{3,19},{4,20},{5,21},{6,22},{7,23},{8,24},{9,... | collective-permute-start | bytes 6291464 | tf_op jit(solution)/shard_map/ppermute | solution.py:15
  309.4 39.8 %all-to-all-start = ((s32[8,1,16]{2,1,0:T(1,128)}), s32[8,1,16]{2,1,0:T(1,128)S(1)}, u32[]{:S(2)}, u32[]{:S(2)}) async-start(s32[8,1,16]{2,1,0:T(1,128)} %bitcast.3), calls=%async_computation | async-start | bytes 8192 | tf_op jit(solution)/shard_map/all_to_all | solution.py:127
  349.2 13.5 %all-to-all-start.1 = ((bf16[8,16,2048]{2,1,0:T(8,128)(2,1)}), bf16[8,16,2048]{2,1,0:T(8,128)(2,1)S(1)}, u32[]{:S(2)}, u32[]{:S(2)}) async-start(bf16[8,16,2048]{2,1,0:T(8,128)(2,1)} %scatter_fusion), calls=%async_computation.3 | async-start | bytes 1048576 | tf_op jit(solution)/shard_map/all_to_all | solution.py:126
Sparse Core Ops, SparseCore 0:
  28.6 54.9 reduce-scatter.2
Sparse Core Ops, SparseCore 1:
  30.5 48.9 all-gather.6
  86.2 17.6 all-gather.4
  111.1 67.5 all-gather.8
  301.4 31.0 reduce-scatter.4
